TPU v7x, 32 devices: a whole 2x2x4 slice. The times are simulated.
32 devices in a mesh: batch: 8 (over z, core), vocab: 4 (over y, x).
Axes of the slice: x: 2, y: 2, z: 4, core: 2. Of those that a mesh axis runs over, the one named last changes fastest.
Arguments:
- window_ids: int32 [3, 16, 8], P(None, 'batch'), may hold values from 0 to 16383
- pool_ids: int32 [3, 16, 8], P(None, 'batch'), may hold values from 0 to 16383
- accepted: int32 [2, 16], P(None, 'batch'), may hold values from 1 to 8
- converged: int32 [2, 16], P(None, 'batch'), may hold values 0 or 1
- cache_lens: int32 [16], P('batch'), may hold values from 1 to 128
- table: bfloat16 [16384, 4608], P(('batch', 'vocab')), may hold values from -0.29882812 to 0.29882812
- attn_gain: float32 [4608], replicated, may hold values from 0.25 to 1.75
- post_gain: float32 [4608], replicated, may hold values from 0.25 to 1.75
- final_gain: float32 [4608], replicated, may hold values from 0.25 to 1.75
- w_query: bfloat16 [4608, 1024], P(None, 'vocab'), may hold values from -0.09375 to 0.09375
- w_key: bfloat16 [4608, 512], P(None, 'vocab'), may hold values from -0.09375 to 0.09375
- w_value: bfloat16 [4608, 512], P(None, 'vocab'), may hold values from -0.09375 to 0.09375
- w_out: bfloat16 [1024, 4608], P('vocab'), may hold values from -0.1875 to 0.1875
- cache_keys: bfloat16 [16, 4, 128, 128], P('batch', 'vocab'), may hold values from -6 to 6
- cache_values: bfloat16 [16, 4, 128, 128], P('batch', 'vocab'), may hold values from -6 to 6
Outputs:
- log_total: float32 [3, 16, 8], P(None, 'batch')
- best_logit: float32 [3, 16, 8], P(None, 'batch')
- pool_score: float32 [3, 16, 8], P(None, 'batch')
Inputs may be any that keep to these rules, and one draw needn't show every extreme that they name: `converged`: 1 marks a window at its fixed point, whose tokens are all accepted.
All inputs are finite; a program needn't handle non-finite values. No bound on the sum of `converged` on one device may be relied on, other than what follows from the above.
Results may differ from a plain program's by a relative error of at most 0.00036.
Values may be sent and summed in bfloat16 or wider, within the bound.
No kernel may reach another device: no remote copies, remote signals or barrier semaphores. Data moves between devices by JAX's collectives and lax.ppermute only.
A program may use at most 128 MiB of HBM per device.

v0:
```python
import math
import jax
import jax.numpy as jnp
from jax import lax
from jax.sharding import PartitionSpec as P

epsilon = 1e-06
query_scalar = 144.0
score_cap = 50.0
logit_cap = 30.0


def normalize(values_in, gain):
    return (
        values_in
        * lax.rsqrt(jnp.mean(values_in * values_in, axis=-1, keepdims=True) + epsilon)
        * gain
    )


def rotate(values_in, positions):
    half_size = values_in.shape[-1] // 2
    freqs = 10000.0 ** (-jnp.arange(half_size, dtype=jnp.float32) / half_size)
    angles = positions.astype(jnp.float32)[..., None] * freqs
    cosine = jnp.cos(angles)
    sine = jnp.sin(angles)
    first_half = values_in[..., :half_size]
    second_half = values_in[..., half_size:]
    return jnp.concatenate(
        [first_half * cosine - second_half * sine, second_half * cosine + first_half * sine],
        axis=-1,
    )


def attend(queries, key_rows, value_rows, visible):
    scores = jnp.einsum("bwhgd,bhld->bhgwl", queries, key_rows, preferred_element_type=jnp.float32)
    scores = score_cap * jnp.tanh(scores / score_cap)
    weights = jnp.where(visible[:, None, None], jnp.exp(scores), 0.0)
    weight_sum = jnp.sum(weights, axis=-1, keepdims=True)
    rounded = lax.optimization_barrier(weights.astype(jnp.bfloat16))
    summed = jnp.einsum(
        "bhgwl,bhld->bwhgd", rounded, value_rows, preferred_element_type=jnp.float32
    )
    return (summed / jnp.moveaxis(weight_sum, 3, 1)).astype(jnp.bfloat16)


def per_device(
    window_ids,
    pool_ids,
    accepted,
    converged,
    cache_lens,
    table,
    attn_gain,
    post_gain,
    final_gain,
    w_query,
    w_key,
    w_value,
    w_out,
    cache_keys,
    cache_values,
):
    iter_count, local_batch, width = window_ids.shape
    model_width = table.shape[1]
    vocab_rows = table.shape[0]
    head_size = cache_keys.shape[3]
    kv_local = cache_keys.shape[1]
    cache_slots = cache_keys.shape[2]
    local_rows = local_batch * width
    vocab_devices = lax.axis_size("vocab")
    batch_index = lax.axis_index("batch")
    vocab_index = lax.axis_index("vocab")
    all_windows, all_pools = (
        lax.all_gather(window_ids, "batch", axis=1, tiled=True),
        lax.all_gather(pool_ids, "batch", axis=1, tiled=True),
    )
    total_batch = all_windows.shape[1]
    first_id = (batch_index * vocab_devices + vocab_index) * vocab_rows
    ordered = jnp.transpose(all_windows, (1, 2, 0)) - first_id
    inside = (ordered >= 0) & (ordered < vocab_rows)
    looked_up = jnp.take(table, jnp.clip(ordered, 0, vocab_rows - 1), axis=0)
    lookup_terms = jnp.where(inside[..., None], looked_up.astype(jnp.float32), 0.0)
    column_rows = lax.psum_scatter(
        lookup_terms.astype(jnp.bfloat16), "batch", scatter_dimension=0, tiled=True
    )
    embedded_all = lax.psum(column_rows, "vocab").astype(jnp.float32)
    taken = jnp.where(converged == 1, width, accepted)
    offset = cache_lens
    slots = jnp.arange(width, dtype=jnp.int32)
    cache_visible = (
        jnp.arange(cache_slots, dtype=jnp.int32)[None, None, :] < cache_lens[:, None, None]
    )
    own_visible = slots[None, None, :] <= slots[None, :, None]
    key_list = [cache_keys]
    value_list = [cache_values]
    mask_list = [jnp.broadcast_to(cache_visible, (local_batch, width, cache_slots))]
    vocab_iota = jnp.arange(vocab_rows, dtype=jnp.int32)
    totals_out = []
    best_out = []
    score_out = []
    for step in range(iter_count):
        embedded = embedded_all[:, :, step] * math.sqrt(model_width)
        normed = (
            normalize(embedded, attn_gain).astype(jnp.bfloat16).reshape(local_rows, model_width)
        )
        positions = (offset[:, None] + slots[None, :])[:, :, None]
        queries = jnp.dot(normed, w_query, preferred_element_type=jnp.float32).reshape(
            local_batch, width, 2 * kv_local, head_size
        )
        queries = (
            (rotate(queries, positions) / math.sqrt(query_scalar))
            .astype(jnp.bfloat16)
            .reshape(local_batch, width, kv_local, 2, head_size)
        )
        keys_now = jnp.dot(normed, w_key, preferred_element_type=jnp.float32).reshape(
            local_batch, width, kv_local, head_size
        )
        keys_now = rotate(keys_now, positions).astype(jnp.bfloat16).transpose(0, 2, 1, 3)
        values_now = jnp.dot(normed, w_value, preferred_element_type=jnp.float32).reshape(
            local_batch, width, kv_local, head_size
        )
        values_now = values_now.astype(jnp.bfloat16).transpose(0, 2, 1, 3)
        all_keys = jnp.concatenate(key_list + [keys_now], axis=2)
        all_values = jnp.concatenate(value_list + [values_now], axis=2)
        visible = jnp.concatenate(
            mask_list + [jnp.broadcast_to(own_visible, (local_batch, width, width))], axis=2
        )
        attended = attend(queries, all_keys, all_values, visible).reshape(
            local_rows, 2 * kv_local * head_size
        )
        branch = jnp.dot(attended, w_out, preferred_element_type=jnp.float32)
        residual = embedded.reshape(local_rows, model_width)
        whole_branch = lax.psum(branch, "vocab")
        hidden = residual + normalize(whole_branch, post_gain)
        final_rows = normalize(hidden, final_gain).astype(jnp.bfloat16)
        pool_local = all_pools[step].reshape(total_batch * width) - first_id
        raw_logits = lax.dot_general(
            lax.all_gather(final_rows, "batch", axis=0, tiled=True),
            table,
            (((1,), (1,)), ((), ())),
            preferred_element_type=jnp.float32,
        )
        logits = logit_cap * jnp.tanh(raw_logits / logit_cap)
        exp_sums = jnp.sum(jnp.exp(logits), axis=-1)
        largest = jnp.max(logits, axis=-1)
        chosen = jnp.sum(
            jnp.where(vocab_iota[None, :] == pool_local[:, None], logits, 0.0), axis=-1
        )
        own_start = batch_index * local_rows
        sums_column, picks_column = (
            lax.psum_scatter(exp_sums, "batch", scatter_dimension=0, tiled=True),
            lax.psum_scatter(chosen, "batch", scatter_dimension=0, tiled=True),
        )
        sums_own, picks_own = lax.psum((sums_column, picks_column), "vocab")
        tops_joint = lax.pmax(largest, ("batch", "vocab"))
        tops_own = lax.dynamic_slice_in_dim(tops_joint, own_start, local_rows)
        log_sum = jnp.log(sums_own)
        totals_out.append(log_sum.reshape(local_batch, width))
        best_out.append(tops_own.reshape(local_batch, width))
        score_out.append((picks_own - log_sum).reshape(local_batch, width))
        if step + 1 < iter_count:
            key_list.append(keys_now)
            value_list.append(values_now)
            mask_list.append(
                jnp.broadcast_to(
                    slots[None, None, :] < taken[step][:, None, None], (local_batch, width, width)
                )
            )
            offset = offset + taken[step]
    return (jnp.stack(totals_out), jnp.stack(best_out), jnp.stack(score_out))


def solution(mesh):
    return jax.shard_map(
        per_device,
        mesh=mesh,
        in_specs=(
            P(None, "batch", None),
            P(None, "batch", None),
            P(None, "batch"),
            P(None, "batch"),
            P("batch"),
            P(("batch", "vocab"), None),
            P(),
            P(),
            P(),
            P(None, "vocab"),
            P(None, "vocab"),
            P(None, "vocab"),
            P("vocab", None),
            P("batch", "vocab", None, None),
            P("batch", "vocab", None, None),
        ),
        out_specs=(P(None, "batch", None), P(None, "batch", None), P(None, "batch", None)),
        check_vma=False,
    )
```

profile of v0, /device:TPU:10, one launch (start us, length us, event | category | flops | bytes accessed | tf_op | source)
XLA Modules:
  0.0 360.0 jit_solution(6029630634133774123)
XLA Ops:
  8.1 14.3 %all_gather.15 = s32[3,16,8]{2,0,1:T(4,128)S(1)} all-gather(s32[3,2,8]{2,0,1:T(4,128)S(1)} %copy.76), channel_id=1, replica_groups=mesh['batch'=8,'vocab'=4] {'batch'}, dimensions={1}, use_global_device_ids=true | all-gather | bytes 1728 | tf_op jit(solution)/shard_map/all_gather | solution.py:75
  22.8 12.2 %gather_fusion = bf16[384,4608]{1,0:T(8,128)(2,1)} fusion(bf16[512,4608]{1,0:T(8,128)(2,1)} %param.20, s32[1024]{0:T(1024)S(1)} %pad_clamp_fusion), kind=kCustom, calls=%fused_computation | custom fusion | bytes 7079424 | tf_op jit(solution)/shard_map/jit(_take)/gather | solution.py:82
  35.0 7.3 %reshape.718 = bf16[16,8,3,4608]{3,2,1,0:T(4,128)(2,1)} reshape(bf16[384,4608]{1,0:T(8,128)(2,1)} %gather_fusion) | data formatting | bytes 7077888 | tf_op jit(solution)/shard_map/jit(_take)/gather | solution.py:82
  42.4 6.3 %select_convert_fusion = bf16[16,8,3,4608]{3,1,2,0:T(8,128)(2,1)} fusion(bf16[16,8,3,4608]{3,2,1,0:T(4,128)(2,1)} %reshape.718, pred[16,8,3]{1,2,0:T(4,128)(4,1)S(1)} %copy.79, pred[16,8,3]{1,2,0:T(4,128)(4,1)S(1)} %copy.78), kind=kLoop, calls=%fused_computation.1 | loop fusion | flops 7077888 | bytes 7078656 | tf_op jit(solution)/shard_map/convert_element_type | solution.py:85
  48.8 4.3 %copy.102 = bf16[256,4608]{1,0:T(8,128)(2,1)} copy(bf16[256,4608]{0,1:T(8,128)(2,1)} %bitcast.314) | data formatting | bytes 4718592 | tf_op jit(solution)/shard_map/dot_general | solution.py:108
  53.7 36.1 %reduce-scatter.2.cloned.1.call-done = bf16[2,8,3,4608]{3,1,2,0:T(8,128)(2,1)} async-done(((bf16[16,8,3,4608]{3,1,2,0:T(8,128)(2,1)}), bf16[2,8,3,4608]{3,1,2,0:T(8,128)(2,1)}) %reduce-scatter.2.cloned.1.call-update) | async-done | bytes 442384 | tf_op jit(solution)/shard_map/reduce_scatter | solution.py:84
  89.8 1.8 copy.82
  92.1 47.6 %all-reduce.13.cloned.1.call-done = bf16[2,8,3,4608]{3,1,0,2:T(8,128)(2,1)} async-done(((bf16[2,8,3,4608]{3,1,0,2:T(8,128)(2,1)}), bf16[2,8,3,4608]{3,1,0,2:T(8,128)(2,1)}) %all-reduce.13.cloned.1.call-update) | async-done | bytes 442384 | tf_op jit(solution)/shard_map/psum | solution.py:87
  141.1 1.6 fusion.45
  142.7 1.7 fusion.48
  151.1 1.2 fusion.70
  152.4 1.2 fusion.69
  153.7 50.5 %all-reduce.15.cloned.1.call-done = (f32[16,4608]{1,0:T(8,128)}, f32[16,4608]{1,0:T(8,128)}, f32[16,4608]{1,0:T(8,128)}) async-done(((f32[16,4608]{1,0:T(8,128)}, f32[16,4608]{1,0:T(8,128)}, f32[16,4608]{1,0:T(8,128)}), (f32[16,4608]{1,0:T(8,128)}, f32[16,4608]{1,0:T(8,128)}, f32[16,4608]{1,0:T(8,128)})) %all-reduce.15.cloned.1.call-update) | async-done | bytes 884752 | tf_op jit(solution)/shard_map/psum | solution.py:134
  207.7 1.5 multiply_reduce_fusion.4
  211.5 14.2 %all_gather.19 = s32[3,16,8]{2,0,1:T(4,128)S(1)} all-gather(s32[3,2,8]{2,0,1:T(4,128)S(1)} %copy.92), channel_id=1, replica_groups=mesh['batch'=8,'vocab'=4] {'batch'}, dimensions={1}, use_global_device_ids=true | all-gather | bytes 1728 | tf_op jit(solution)/shard_map/all_gather | solution.py:76
  227.3 5.9 %all-gather.4.cloned.1.call-done = bf16[128,4608]{1,0:T(8,128)(2,1)} async-done(((bf16[16,4608]{1,0:T(8,128)(2,1)}), bf16[128,4608]{1,0:T(8,128)(2,1)}) %all-gather.4.cloned.1.call-update) | async-done | bytes 1179664 | tf_op jit(solution)/shard_map/all_gather | solution.py:139
  233.2 4.5 %select_reduce_fusion.2 = (f32[128]{0:T(128)S(1)}, f32[128]{0:T(128)S(1)}, f32[128]{0:T(128)S(1)}) fusion(s32[128]{0:T(128)S(1)} %sub.79, bf16[128,4608]{1,0:T(8,128)(2,1)} %all-gather.4.cloned.1.call-done, bf16[512,4608]{1,0:T(8,128)(2,1)} %param.20), kind=kOutput, calls=%fused_computation.103 | convolution fusion | flops 604438144 | bytes 5900288 | tf_op jit(solution)/shard_map/dot_general | solution.py:138
  237.7 19.4 %all-gather.6.cloned.1.call-done = bf16[128,4608]{1,0:T(8,128)(2,1)} async-done(((bf16[16,4608]{1,0:T(8,128)(2,1)}), bf16[128,4608]{1,0:T(8,128)(2,1)}) %all-gather.6.cloned.1.call-update) | async-done | bytes 1179664 | tf_op jit(solution)/shard_map/all_gather | solution.py:139
  257.1 4.5 %select_reduce_fusion.1 = (f32[128]{0:T(128)S(1)}, f32[128]{0:T(128)S(1)}, f32[128]{0:T(128)S(1)}) fusion(s32[128]{0:T(128)S(1)} %sub.82, bf16[128,4608]{1,0:T(8,128)(2,1)} %all-gather.6.cloned.1.call-done, bf16[512,4608]{1,0:T(8,128)(2,1)} %param.20), kind=kOutput, calls=%fused_computation.101 | convolution fusion | flops 604438144 | bytes 5900288 | tf_op jit(solution)/shard_map/dot_general | solution.py:138
  261.6 19.5 %all-gather.8.cloned.1.call-done = bf16[128,4608]{1,0:T(8,128)(2,1)} async-done(((bf16[16,4608]{1,0:T(8,128)(2,1)}), bf16[128,4608]{1,0:T(8,128)(2,1)}) %all-gather.8.cloned.1.call-update) | async-done | bytes 1179664 | tf_op jit(solution)/shard_map/all_gather | solution.py:139
  281.0 4.5 %select_reduce_fusion = (f32[128]{0:T(128)S(1)}, f32[128]{0:T(128)S(1)}, f32[128]{0:T(128)S(1)}) fusion(s32[128]{0:T(128)S(1)} %sub.85, bf16[128,4608]{1,0:T(8,128)(2,1)} %all-gather.8.cloned.1.call-done, bf16[512,4608]{1,0:T(8,128)(2,1)} %param.20), kind=kOutput, calls=%fused_computation.99 | convolution fusion | flops 604438144 | bytes 5900288 | tf_op jit(solution)/shard_map/dot_general | solution.py:138
  285.5 12.1 %all-reduce.7 = (f32[128]{0:T(128)S(1)}, f32[128]{0:T(128)S(1)}, f32[128]{0:T(128)S(1)}, f32[128]{0:T(128)S(1)}, f32[128]{0:T(128)S(1)}, /*index=5*/f32[128]{0:T(128)S(1)}) all-reduce(f32[128]{0:T(128)S(1)} %get-tuple-element.17, f32[128]{0:T(128)S(1)} %get-tuple-element.14, ...), channel_id=5, replica_groups=mesh['batch'=8,'vocab'=4] {'batch'}, use_global_device_ids=true, to_apply=%region_24.25.clone | all-reduce | flops 768 | bytes 6144
  298.1 8.0 %all-reduce.8 = (f32[16]{0:T(128)S(1)}, f32[16]{0:T(128)S(1)}, f32[16]{0:T(128)S(1)}, f32[16]{0:T(128)S(1)}, f32[16]{0:T(128)S(1)}, /*index=5*/f32[16]{0:T(128)S(1)}) all-reduce(f32[16]{0:T(128)S(1)} %dynamic-slice.5, f32[16]{0:T(128)S(1)} %dynamic-slice.3, f32[16]{0:T(128)S(1)} %dynamic-slice.1, ...), channel_id=1, replica_groups=mesh['batch'=8,'vocab'=4] {'vocab'}, use_global_device_ids=true, to_apply=%region_25.26 | all-reduce | flops 96 | bytes 768 | tf_op jit(solution)/shard_map/psum | solution.py:155
  306.4 44.3 %all-reduce.6 = (f32[128]{0:T(128)S(1)}, f32[128]{0:T(128)S(1)}, f32[128]{0:T(128)S(1)}) all-reduce(f32[128]{0:T(128)S(1)} %get-tuple-element.16, f32[128]{0:T(128)S(1)} %get-tuple-element.13, f32[128]{0:T(128)S(1)} %get-tuple-element.10), channel_id=1, replica_groups=mesh['batch'=8,'vocab'=4] {'batch','vocab'}, use_global_device_ids=true, to_apply=%region_31.32 | all-reduce | flops 384 | bytes 3072 | tf_op jit(solution)/shard_map/pmax | solution.py:156
  (131 shorter events, 20.4 us)
Async XLA Ops:
  7.2 142.7 %copy-start = (bf16[256,4608]{1,0:T(8,128)(2,1)S(1)}, bf16[256,4608]{1,0:T(8,128)(2,1)}, u32[]{:S(2)}) copy-start(bf16[256,4608]{1,0:T(8,128)(2,1)} %param.27) | copy-start | bytes 7077892
  7.2 82.6 %reduce-scatter.2.cloned.1.call-start = ((), (), s32[]{:S(2)}) async-start(), calls=%async_computation.1 | async-start | bytes 3981312 | tf_op jit(solution)/shard_map/reduce_scatter | solution.py:84
  48.7 90.9 %all-reduce.13.cloned.1.call-start = ((), (), s32[]{:S(2)}) async-start(), calls=%async_computation.2 | async-start | bytes 884736 | tf_op jit(solution)/shard_map/psum | solution.py:87
  48.8 4.4 %copy-start.14 = (s32[2]{0:T(128)S(1)}, s32[2]{0:T(128)}, u32[]{:S(2)}) copy-start(s32[2]{0:T(128)} %param.19) | copy-start | bytes 28
  48.8 4.5 %copy-start.12 = (s32[2,2]{1,0:T(2,128)S(1)}, s32[2,2]{1,0:T(2,128)}, u32[]{:S(2)}) copy-start(s32[2,2]{1,0:T(2,128)} %param.17) | copy-start | bytes 52
  48.8 4.5 %copy-start.13 = (s32[2,2]{1,0:T(2,128)S(1)}, s32[2,2]{1,0:T(2,128)}, u32[]{:S(2)}) copy-start(s32[2,2]{1,0:T(2,128)} %param.18) | copy-start | bytes 52
  53.2 87.9 %copy-start.4 = (f32[4608]{0:T(1024)S(1)}, f32[4608]{0:T(1024)}, u32[]{:S(2)}) copy-start(f32[4608]{0:T(1024)} %param.21) | copy-start | bytes 55300
  91.6 112.6 %all-reduce.15.cloned.1.call-start = ((), (), s32[]{:S(2)}) async-start(), calls=%async_computation.6 | async-start | bytes 1769472 | tf_op jit(solution)/shard_map/psum | solution.py:134
  139.7 4.7 %copy-start.3 = (bf16[4608,128]{1,0:T(8,128)(2,1)S(1)}, bf16[4608,128]{1,0:T(8,128)(2,1)}, u32[]{:S(2)}) copy-start(bf16[4608,128]{1,0:T(8,128)(2,1)} %param.26) | copy-start | bytes 3538948
  142.6 2.4 copy-start.2
  144.7 1.7 copy-start.1
  147.1 1.7 copy-start.15
  147.8 2.1 copy-start.8
  152.4 55.3 %copy-start.9 = (f32[4608]{0:T(1024)S(1)}, f32[4608]{0:T(1024)}, u32[]{:S(2)}) copy-start(f32[4608]{0:T(1024)} %param.22) | copy-start | bytes 55300
  153.6 55.6 %copy-start.10 = (f32[4608]{0:T(1024)S(1)}, f32[4608]{0:T(1024)}, u32[]{:S(2)}) copy-start(f32[4608]{0:T(1024)} %param.23) | copy-start | bytes 55300
  153.6 79.6 %all-gather.4.cloned.1.call-start = ((), (), s32[]{:S(2)}) async-start(), calls=%async_computation.3 | async-start | bytes 1327104 | tf_op jit(solution)/shard_map/all_gather | solution.py:139
  204.2 5.1 %copy-start.5 = (f32[16,4608]{1,0:T(8,128)S(1)}, f32[16,4608]{1,0:T(8,128)}, u32[]{:S(2)}) copy-start(f32[16,4608]{1,0:T(8,128)} %get-tuple-element.36) | copy-start | bytes 884740
  204.2 5.1 %copy-start.6 = (f32[16,4608]{1,0:T(8,128)S(1)}, f32[16,4608]{1,0:T(8,128)}, u32[]{:S(2)}) copy-start(f32[16,4608]{1,0:T(8,128)} %get-tuple-element.37) | copy-start | bytes 884740
  204.2 5.1 %copy-start.7 = (f32[16,4608]{1,0:T(8,128)S(1)}, f32[16,4608]{1,0:T(8,128)}, u32[]{:S(2)}) copy-start(f32[16,4608]{1,0:T(8,128)} %get-tuple-element.38) | copy-start | bytes 884740
  206.5 4.9 %copy-start.11 = (s32[3,2,8]{2,1,0:T(2,128)S(1)}, s32[3,2,8]{2,1,0:T(2,128)}, u32[]{:S(2)}) copy-start(s32[3,2,8]{2,1,0:T(2,128)} %param.16) | copy-start | bytes 580
  207.6 18.4 %copy-start.16 = (u32[32]{0:T(128)S(1)}, u32[32]{0:T(128)}, u32[]{:S(2)}) copy-start(u32[32]{0:T(128)} %constant.94) | copy-start | bytes 388
  210.3 46.8 %all-gather.6.cloned.1.call-start = ((), (), s32[]{:S(2)}) async-start(), calls=%async_computation.4 | async-start | bytes 1327104 | tf_op jit(solution)/shard_map/all_gather | solution.py:139
  210.9 70.2 %all-gather.8.cloned.1.call-start = ((), (), s32[]{:S(2)}) async-start(), calls=%async_computation.5 | async-start | bytes 1327104 | tf_op jit(solution)/shard_map/all_gather | solution.py:139
Sparse Core Ops, SparseCore 0:
  48.9 40.8 reduce-scatter.1
  92.8 46.8 all-reduce.12
  153.7 50.3 all-reduce.14
  210.4 22.7 all-gather.3
  234.7 22.3 all-gather.5
  258.6 22.4 all-gather.7
where the time goes:
time: 361 us; the launch traced here: 360 us
  waiting for transfers between devices  180 us (50%)
  blocking collectives  92.9 us (26%)
  local copies, waits for them, and re-layouts  30 us (8%)
  matrix products  24.9 us (7%)
  other arithmetic  16.6 us (5%)
  between operations  15.1 us (4%)
    psum x1, waiting for transfers between devices, per_device(): whole_branch = lax.psum(branch, 'vocab')  50.5 us
    psum x1, waiting for transfers between devices, per_device(): embedded_all = lax.psum(column_rows, 'vocab').astype(jnp.float32)  47.6 us
    all_gather x3, waiting for transfers between devices, per_device(): lax.all_gather(final_rows, 'batch', axis=0, tiled=True)  44.7 us
    pmax x1, blocking collectives, per_device(): tops_joint = lax.pmax(largest, ('batch', 'vocab'))  44.3 us
    reduce_scatter x1, waiting for transfers between devices, per_device(): lax.psum_scatter(lookup_terms.astype(jnp.bfloat16), 'batch', scatter_dime...  36.1 us
    gather x2, local copies, waits for them, and re-layouts, per_device(): looked_up = jnp.take(table, jnp.clip(ordered, 0, vocab_rows - 1), axis=0)  19.4 us
    all_gather x1, blocking collectives, per_device(): lax.all_gather(window_ids, 'batch', axis=1, tiled=True)  14.3 us
    all_gather x1, blocking collectives, per_device(): lax.all_gather(pool_ids, 'batch', axis=1, tiled=True)  14.2 us
  transfers between devices with their start and end apart: 6, of which 6 were waited for; matrix products, arithmetic and copies ran while one was open for 4% of the time, Pallas kernels for 0%

commit v1 on v0

--- a/solution.py
+++ b/solution.py
@@ -84,7 +84,7 @@
     column_rows = lax.psum_scatter(
         lookup_terms.astype(jnp.bfloat16), "batch", scatter_dimension=0, tiled=True
     )
-    embedded_all = lax.psum(column_rows, "vocab").astype(jnp.float32)
+    embedded_all = jnp.sum(lax.all_gather(column_rows, "vocab"), axis=0).astype(jnp.float32)
     taken = jnp.where(converged == 1, width, accepted)
     offset = cache_lens
     slots = jnp.arange(width, dtype=jnp.int32)

time: 361 us -> 347 us (0.961)
  waiting for transfers between devices: 180 us -> 168 us
    psum x1 -> x0, waiting for transfers between devices: 47.6 us -> none  [per_device(): embedded_all = lax.psum(column_rows, 'vocab').astype(jnp.float32)]
    all_gather x0 -> x1, waiting for transfers between devices: none -> 31.2 us  [per_device(): lax.all_gather(column_rows, 'vocab')]
    reduce_scatter x1, waiting for transfers between devices: 36.1 us -> 41 us  [per_device(): lax.psum_scatter(lookup_terms.astype(jnp.bfloat16), 'batch', scatter_dime...]
where the time goes in v1:
time: 347 us
  waiting for transfers between devices  168 us (48%)
  blocking collectives  92.9 us (27%)
  local copies, waits for them, and re-layouts  29 us (8%)
  matrix products  22.1 us (6%)
  other arithmetic  18.6 us (5%)
  between operations  15.1 us (4%)
    psum x1, waiting for transfers between devices, per_device(): whole_branch = lax.psum(branch, 'vocab')  50.4 us
    all_gather x3, waiting for transfers between devices, per_device(): lax.all_gather(final_rows, 'batch', axis=0, tiled=True)  44.7 us
    pmax x1, blocking collectives, per_device(): tops_joint = lax.pmax(largest, ('batch', 'vocab'))  44.3 us
    reduce_scatter x1, waiting for transfers between devices, per_device(): lax.psum_scatter(lookup_terms.astype(jnp.bfloat16), 'batch', scatter_dime...  41 us
    all_gather x1, waiting for transfers between devices, per_device(): lax.all_gather(column_rows, 'vocab')  31.2 us
    gather x2, local copies, waits for them, and re-layouts, per_device(): looked_up = jnp.take(table, jnp.clip(ordered, 0, vocab_rows - 1), axis=0)  19.4 us
    all_gather x1, blocking collectives, per_device(): lax.all_gather(window_ids, 'batch', axis=1, tiled=True)  14.3 us
    all_gather x1, blocking collectives, per_device(): lax.all_gather(pool_ids, 'batch', axis=1, tiled=True)  14.2 us
  transfers between devices with their start and end apart: 6, of which 6 were waited for; matrix products, arithmetic and copies ran while one was open for 4% of the time, Pallas kernels for 0%

profile of v1, /device:TPU:10, one launch (start us, length us, event | category | flops | bytes accessed | tf_op | source)
XLA Modules:
  0.0 346.6 jit_solution(12664887982420587214)
XLA Ops:
  8.1 14.3 %all_gather.21 = s32[3,16,8]{2,0,1:T(4,128)S(1)} all-gather(s32[3,2,8]{2,0,1:T(4,128)S(1)} %copy.81), channel_id=1, replica_groups=mesh['batch'=8,'vocab'=4] {'batch'}, dimensions={1}, use_global_device_ids=true | all-gather | bytes 1728 | tf_op jit(solution)/shard_map/all_gather | solution.py:75
  22.8 12.2 %gather_fusion = bf16[384,4608]{1,0:T(8,128)(2,1)} fusion(bf16[512,4608]{1,0:T(8,128)(2,1)} %param.20, s32[1024]{0:T(1024)S(1)} %pad_clamp_fusion), kind=kCustom, calls=%fused_computation | custom fusion | bytes 7079424 | tf_op jit(solution)/shard_map/jit(_take)/gather | solution.py:82
  35.0 7.3 %reshape.718 = bf16[16,8,3,4608]{3,2,1,0:T(4,128)(2,1)} reshape(bf16[384,4608]{1,0:T(8,128)(2,1)} %gather_fusion) | data formatting | bytes 7077888 | tf_op jit(solution)/shard_map/jit(_take)/gather | solution.py:82
  42.4 6.3 %select_convert_fusion = bf16[16,8,3,4608]{3,1,2,0:T(8,128)(2,1)} fusion(bf16[16,8,3,4608]{3,2,1,0:T(4,128)(2,1)} %reshape.718, pred[16,8,3]{1,2,0:T(4,128)(4,1)S(1)} %copy.84, pred[16,8,3]{1,2,0:T(4,128)(4,1)S(1)} %copy.83), kind=kLoop, calls=%fused_computation.1 | loop fusion | flops 7077888 | bytes 7078656 | tf_op jit(solution)/shard_map/convert_element_type | solution.py:85
  48.8 41.0 %reduce-scatter.2.cloned.1.call-done = bf16[2,8,3,4608]{3,1,2,0:T(8,128)(2,1)} async-done(((bf16[16,8,3,4608]{3,1,2,0:T(8,128)(2,1)}), bf16[2,8,3,4608]{3,1,2,0:T(8,128)(2,1)}) %reduce-scatter.2.cloned.1.call-update) | async-done | bytes 442384 | tf_op jit(solution)/shard_map/reduce_scatter | solution.py:84
  90.1 4.3 %copy.111 = bf16[256,4608]{1,0:T(8,128)(2,1)} copy(bf16[256,4608]{0,1:T(8,128)(2,1)} %bitcast.315) | data formatting | bytes 4718592 | tf_op jit(solution)/shard_map/dot_general | solution.py:108
  95.2 31.2 %all-gather.12.cloned.1.call-done = bf16[8,8,3,4608]{3,1,2,0:T(8,128)(2,1)} async-done(((bf16[2,8,3,4608]{3,1,2,0:T(8,128)(2,1)}), bf16[8,8,3,4608]{3,1,2,0:T(8,128)(2,1)}) %all-gather.12.cloned.1.call-update) | async-done | bytes 1769488 | tf_op jit(solution)/shard_map/all_gather | solution.py:87
  126.4 1.8 reduce_sum.174
  136.6 1.2 fusion.71
  137.9 1.2 fusion.70
  139.1 1.2 fusion.69
  140.4 50.4 %all-reduce.12.cloned.1.call-done = (f32[16,4608]{1,0:T(8,128)}, f32[16,4608]{1,0:T(8,128)}, f32[16,4608]{1,0:T(8,128)}) async-done(((f32[16,4608]{1,0:T(8,128)}, f32[16,4608]{1,0:T(8,128)}, f32[16,4608]{1,0:T(8,128)}), (f32[16,4608]{1,0:T(8,128)}, f32[16,4608]{1,0:T(8,128)}, f32[16,4608]{1,0:T(8,128)})) %all-reduce.12.cloned.1.call-update) | async-done | bytes 884752 | tf_op jit(solution)/shard_map/psum | solution.py:134
  190.8 1.2 multiply_reduce_fusion.1
  194.3 1.5 multiply_reduce_fusion.4
  198.1 14.2 %all_gather.27 = s32[3,16,8]{2,0,1:T(4,128)S(1)} all-gather(s32[3,2,8]{2,0,1:T(4,128)S(1)} %copy.101), channel_id=1, replica_groups=mesh['batch'=8,'vocab'=4] {'batch'}, dimensions={1}, use_global_device_ids=true | all-gather | bytes 1728 | tf_op jit(solution)/shard_map/all_gather | solution.py:76
  214.0 5.9 %all-gather.6.cloned.1.call-done = bf16[128,4608]{1,0:T(8,128)(2,1)} async-done(((bf16[16,4608]{1,0:T(8,128)(2,1)}), bf16[128,4608]{1,0:T(8,128)(2,1)}) %all-gather.6.cloned.1.call-update) | async-done | bytes 1179664 | tf_op jit(solution)/shard_map/all_gather | solution.py:139
  219.8 4.5 %select_reduce_fusion.2 = (f32[128]{0:T(128)S(1)}, f32[128]{0:T(128)S(1)}, f32[128]{0:T(128)S(1)}) fusion(s32[128]{0:T(128)S(1)} %sub.79, bf16[128,4608]{1,0:T(8,128)(2,1)} %all-gather.6.cloned.1.call-done, bf16[512,4608]{1,0:T(8,128)(2,1)} %param.20), kind=kOutput, calls=%fused_computation.106 | convolution fusion | flops 604438144 | bytes 5900288 | tf_op jit(solution)/shard_map/dot_general | solution.py:138
  224.3 19.4 %all-gather.8.cloned.1.call-done = bf16[128,4608]{1,0:T(8,128)(2,1)} async-done(((bf16[16,4608]{1,0:T(8,128)(2,1)}), bf16[128,4608]{1,0:T(8,128)(2,1)}) %all-gather.8.cloned.1.call-update) | async-done | bytes 1179664 | tf_op jit(solution)/shard_map/all_gather | solution.py:139
  243.7 4.5 %select_reduce_fusion.1 = (f32[128]{0:T(128)S(1)}, f32[128]{0:T(128)S(1)}, f32[128]{0:T(128)S(1)}) fusion(s32[128]{0:T(128)S(1)} %sub.82, bf16[128,4608]{1,0:T(8,128)(2,1)} %all-gather.8.cloned.1.call-done, bf16[512,4608]{1,0:T(8,128)(2,1)} %param.20), kind=kOutput, calls=%fused_computation.104 | convolution fusion | flops 604438144 | bytes 5900288 | tf_op jit(solution)/shard_map/dot_general | solution.py:138
  248.2 19.5 %all-gather.10.cloned.1.call-done = bf16[128,4608]{1,0:T(8,128)(2,1)} async-done(((bf16[16,4608]{1,0:T(8,128)(2,1)}), bf16[128,4608]{1,0:T(8,128)(2,1)}) %all-gather.10.cloned.1.call-update) | async-done | bytes 1179664 | tf_op jit(solution)/shard_map/all_gather | solution.py:139
  267.7 4.5 %select_reduce_fusion = (f32[128]{0:T(128)S(1)}, f32[128]{0:T(128)S(1)}, f32[128]{0:T(128)S(1)}) fusion(s32[128]{0:T(128)S(1)} %sub.85, bf16[128,4608]{1,0:T(8,128)(2,1)} %all-gather.10.cloned.1.call-done, bf16[512,4608]{1,0:T(8,128)(2,1)} %param.20), kind=kOutput, calls=%fused_computation.102 | convolution fusion | flops 604438144 | bytes 5900288 | tf_op jit(solution)/shard_map/dot_general | solution.py:138
  272.2 12.1 %all-reduce.7 = (f32[128]{0:T(128)S(1)}, f32[128]{0:T(128)S(1)}, f32[128]{0:T(128)S(1)}, f32[128]{0:T(128)S(1)}, f32[128]{0:T(128)S(1)}, /*index=5*/f32[128]{0:T(128)S(1)}) all-reduce(f32[128]{0:T(128)S(1)} %get-tuple-element.11, f32[128]{0:T(128)S(1)} %get-tuple-element.8, ...), channel_id=6, replica_groups=mesh['batch'=8,'vocab'=4] {'batch'}, use_global_device_ids=true, to_apply=%region_24.25.clone | all-reduce | flops 768 | bytes 6144
  284.7 8.0 %all-reduce.8 = (f32[16]{0:T(128)S(1)}, f32[16]{0:T(128)S(1)}, f32[16]{0:T(128)S(1)}, f32[16]{0:T(128)S(1)}, f32[16]{0:T(128)S(1)}, /*index=5*/f32[16]{0:T(128)S(1)}) all-reduce(f32[16]{0:T(128)S(1)} %dynamic-slice.5, f32[16]{0:T(128)S(1)} %dynamic-slice.3, f32[16]{0:T(128)S(1)} %dynamic-slice.1, ...), channel_id=1, replica_groups=mesh['batch'=8,'vocab'=4] {'vocab'}, use_global_device_ids=true, to_apply=%region_25.26 | all-reduce | flops 96 | bytes 768 | tf_op jit(solution)/shard_map/psum | solution.py:155
  293.0 44.3 %all-reduce.6 = (f32[128]{0:T(128)S(1)}, f32[128]{0:T(128)S(1)}, f32[128]{0:T(128)S(1)}) all-reduce(f32[128]{0:T(128)S(1)} %get-tuple-element.10, f32[128]{0:T(128)S(1)} %get-tuple-element.7, f32[128]{0:T(128)S(1)} %get-tuple-element.4), channel_id=1, replica_groups=mesh['batch'=8,'vocab'=4] {'batch','vocab'}, use_global_device_ids=true, to_apply=%region_31.32 | all-reduce | flops 384 | bytes 3072 | tf_op jit(solution)/shard_map/pmax | solution.py:156
  (135 shorter events, 19.5 us)
Async XLA Ops:
  7.2 129.4 %copy-start = (bf16[256,4608]{1,0:T(8,128)(2,1)S(1)}, bf16[256,4608]{1,0:T(8,128)(2,1)}, u32[]{:S(2)}) copy-start(bf16[256,4608]{1,0:T(8,128)(2,1)} %param.27) | copy-start | bytes 7077892
  7.2 82.6 %reduce-scatter.2.cloned.1.call-start = ((), (), s32[]{:S(2)}) async-start(), calls=%async_computation.1 | async-start | bytes 3981312 | tf_op jit(solution)/shard_map/reduce_scatter | solution.py:84
  48.7 77.7 %all-gather.12.cloned.1.call-start = ((), (), s32[]{:S(2)}) async-start(), calls=%async_computation.5 | async-start | bytes 2211840 | tf_op jit(solution)/shard_map/all_gather | solution.py:87
  89.8 101.0 %all-reduce.12.cloned.1.call-start = ((), (), s32[]{:S(2)}) async-start(), calls=%async_computation.6 | async-start | bytes 1769472 | tf_op jit(solution)/shard_map/psum | solution.py:134
  90.0 4.4 %copy-start.14 = (s32[2]{0:T(128)S(1)}, s32[2]{0:T(128)}, u32[]{:S(2)}) copy-start(s32[2]{0:T(128)} %param.19) | copy-start | bytes 28
  90.0 4.5 %copy-start.12 = (s32[2,2]{1,0:T(2,128)S(1)}, s32[2,2]{1,0:T(2,128)}, u32[]{:S(2)}) copy-start(s32[2,2]{1,0:T(2,128)} %param.17) | copy-start | bytes 52
  90.1 4.5 %copy-start.13 = (s32[2,2]{1,0:T(2,128)S(1)}, s32[2,2]{1,0:T(2,128)}, u32[]{:S(2)}) copy-start(s32[2,2]{1,0:T(2,128)} %param.18) | copy-start | bytes 52
  126.4 2.8 copy-start.7
  128.2 2.0 copy-start.2
  130.2 1.3 copy-start.3
  131.5 1.7 copy-start.1
  133.8 1.7 copy-start.15
  134.5 2.1 copy-start.8
  139.1 55.2 %copy-start.9 = (f32[4608]{0:T(1024)S(1)}, f32[4608]{0:T(1024)}, u32[]{:S(2)}) copy-start(f32[4608]{0:T(1024)} %param.22) | copy-start | bytes 55300
  140.3 55.5 %copy-start.10 = (f32[4608]{0:T(1024)S(1)}, f32[4608]{0:T(1024)}, u32[]{:S(2)}) copy-start(f32[4608]{0:T(1024)} %param.23) | copy-start | bytes 55300
  140.4 79.5 %all-gather.6.cloned.1.call-start = ((), (), s32[]{:S(2)}) async-start(), calls=%async_computation.2 | async-start | bytes 1327104 | tf_op jit(solution)/shard_map/all_gather | solution.py:139
  190.8 5.1 %copy-start.4 = (f32[16,4608]{1,0:T(8,128)S(1)}, f32[16,4608]{1,0:T(8,128)}, u32[]{:S(2)}) copy-start(f32[16,4608]{1,0:T(8,128)} %get-tuple-element.33) | copy-start | bytes 884740
  190.8 5.1 %copy-start.5 = (f32[16,4608]{1,0:T(8,128)S(1)}, f32[16,4608]{1,0:T(8,128)}, u32[]{:S(2)}) copy-start(f32[16,4608]{1,0:T(8,128)} %get-tuple-element.34) | copy-start | bytes 884740
  190.8 5.1 %copy-start.6 = (f32[16,4608]{1,0:T(8,128)S(1)}, f32[16,4608]{1,0:T(8,128)}, u32[]{:S(2)}) copy-start(f32[16,4608]{1,0:T(8,128)} %get-tuple-element.35) | copy-start | bytes 884740
  193.2 4.9 %copy-start.11 = (s32[3,2,8]{2,1,0:T(2,128)S(1)}, s32[3,2,8]{2,1,0:T(2,128)}, u32[]{:S(2)}) copy-start(s32[3,2,8]{2,1,0:T(2,128)} %param.16) | copy-start | bytes 580
  194.3 18.4 %copy-start.16 = (u32[32]{0:T(128)S(1)}, u32[32]{0:T(128)}, u32[]{:S(2)}) copy-start(u32[32]{0:T(128)} %constant.96) | copy-start | bytes 388
  196.9 46.8 %all-gather.8.cloned.1.call-start = ((), (), s32[]{:S(2)}) async-start(), calls=%async_computation.3 | async-start | bytes 1327104 | tf_op jit(solution)/shard_map/all_gather | solution.py:139
  197.5 70.2 %all-gather.10.cloned.1.call-start = ((), (), s32[]{:S(2)}) async-start(), calls=%async_computation.4 | async-start | bytes 1327104 | tf_op jit(solution)/shard_map/all_gather | solution.py:139
Sparse Core Ops, SparseCore 0:
  48.9 40.8 reduce-scatter.1
  91.6 34.7 all-gather.11
  140.5 50.3 all-reduce.11
  197.0 22.7 all-gather.5
  221.3 22.3 all-gather.7
  245.2 22.4 all-gather.9
